TPU v7x, 32 devices: a whole 2x2x4 slice. The times are simulated.
32 devices in a mesh: grp: 8 (over y, x, core), fsdp: 4 (over z).
Axes of the slice: x: 2, y: 2, z: 4, core: 2. Of those that a mesh axis runs over, the one named last changes fastest.
Arguments:
- layer_inputs: bfloat16 [8, 2048, 2048], P('grp', 'fsdp'), may hold values from -6 to 6
- key_cotangent: bfloat16 [8, 2048, 768], P('grp', 'fsdp'), may hold values from -0.099609375 to 0.099609375
- key_weights: bfloat16 [2048, 768], P('fsdp'), may hold values from -0.125 to 0.125
- outer_momentum: float32 [2048, 768], P('fsdp'), may hold values from -0.02 to 0.02
- state_codes: int32 [8, 2048, 768], P('grp', 'fsdp'), may hold values from 0 to 255
- first_row_max: float32 [8, 2048], P('grp', 'fsdp'), may hold values from 0.1 to 2
- first_col_max: float32 [8, 768], P('grp'), may hold values from 0.1 to 2
- second_row_max: float32 [8, 2048], P('grp', 'fsdp'), may hold values from 0.1 to 4
- second_col_max: float32 [8, 768], P('grp'), may hold values from 0.1 to 4
Outputs:
- new_weights: float32 [2048, 768], P('fsdp')
- new_momentum: float32 [2048, 768], P('fsdp')
- first_state: bfloat16 [8, 2048, 768], P('grp', 'fsdp')
- second_state: bfloat16 [8, 2048, 768], P('grp', 'fsdp')
- new_first_row_max: float32 [8, 2048], P('grp', 'fsdp')
- new_first_col_max: float32 [8, 768], P('grp')
- new_second_row_max: float32 [8, 2048], P('grp', 'fsdp')
- new_second_col_max: float32 [8, 768], P('grp')
- next_keys: bfloat16 [8, 2048, 768], P('grp', 'fsdp')
All inputs are finite; a program needn't handle non-finite values. Where the computation divides by a largest or mean magnitude, that divisor is 1e-20 or more.
Results may differ from a plain program's by a relative error of at most 0.018.
Values may be sent and summed in bfloat16 or wider, within the bound.
A program may use at most 64 MiB of HBM per device.

v0:
```python
import functools
import jax
import jax.numpy as jnp
from jax import lax
from jax.experimental import pallas as pl
from jax.experimental.pallas import tpu as pltpu
from jax.sharding import PartitionSpec as P

MESH = pl.DeviceIdType.MESH
f32, bf16 = jnp.float32, jnp.bfloat16
beta_one = 0.9
beta_two = 0.95
bias_one = 1.0 - 0.9**10
bias_two = 1.0 - 0.95**10
adam_eps = 1e-08
inner_rate = 0.01
weight_decay = 0.1
outer_rate = 0.7
outer_beta = 0.9
stat_eps = 1e-06
TILE = 16


def to_column(row):
    return jnp.broadcast_to(row, (128, row.shape[1])).T[:, :1]


def to_row(column):
    return jnp.broadcast_to(column, (column.shape[0], 128)).T[:1, :]


def kernel(
    n, G, S, R, PR, NP,
    x_hbm, c_hbm, w_hbm, m_hbm, q_hbm, frm, fcm, srm, scm,
    o_a, o_fs, o_ss, o_frm, o_fcm, o_srm, o_scm, o_k,
    x, ct, w, m, q, tb, rb, pb, rp, av, wf, fn, sn, acc, fcol, scol, frn, srn, ca, cb, cmb,
    ld, ts, tr, ps, pr, as_, ar, gs, gr, hs, hr, cs, cr,
):
    g = lax.axis_index("grp")
    z = lax.axis_index("fsdp")
    rows = S * R
    C = w.shape[1]
    half = R // 2
    h = lax.rem(g, 2)
    mate = g + 1 - 2 * h

    loads = [
        pltpu.make_async_copy(src, dst, ld.at[i])
        for i, (src, dst) in enumerate(
            ((c_hbm, ct), (x_hbm, x), (q_hbm, q), (w_hbm, w), (m_hbm, m))
        )
    ]
    for load in loads:
        load.start()

    barrier = pltpu.get_barrier_semaphore()
    for d in range(1, G):
        pl.semaphore_signal(
            barrier, inc=1, device_id=(lax.rem(g + d, G), z), device_id_type=MESH
        )
    for d in range(1, n):
        pl.semaphore_signal(
            barrier, inc=1, device_id=(g, lax.rem(z + d, n)), device_id_type=MESH
        )

    for s in range(S):
        block = pl.ds(s * R, R)
        fcol[block, :] = to_column(frm[:, block])
        scol[block, :] = to_column(srm[:, block])
    ca[...] = jnp.zeros_like(ca)
    cb[...] = jnp.zeros_like(cb)

    pl.semaphore_wait(barrier, G - 1 + n - 1)
    loads[0].wait()
    loads[1].wait()

    def term(c, s):
        columns = pl.ds(pl.multiple_of(c * rows + s * R, 128), R)
        return lax.dot_general(
            x[:, columns], ct[...], (((0,), (0,)), ((), ())), preferred_element_type=f32
        )

    def move(s, c, slot, to):
        return pltpu.make_async_remote_copy(
            src_ref=tb.at[s, c], dst_ref=rb.at[s, slot], send_sem=ts.at[s, c],
            recv_sem=tr.at[s, slot], device_id=(g, to), device_id_type=MESH,
        )

    other_z = lax.rem(z + 1, n)

    def stream(s):
        def step(k, carry):
            right = n - 1 - k
            left = k

            @pl.when(right > z)
            def _():
                @pl.when(z == 0)
                def _():
                    tb[s, right] = term(right, s).astype(bf16)

                @pl.when(z > 0)
                def _():
                    own = term(right, s)
                    move(s, right, right, other_z).wait_recv()
                    tb[s, right] = (own + rb[s, right].astype(f32)).astype(bf16)

                move(s, right, right, z + 1).start()

            @pl.when(left < z)
            def _():
                @pl.when(z == n - 1)
                def _():
                    tb[s, left] = term(left, s).astype(bf16)

                @pl.when(z < n - 1)
                def _():
                    own = term(left, s)
                    move(s, left, left, other_z).wait_recv()
                    tb[s, left] = (own + rb[s, left].astype(f32)).astype(bf16)

                move(s, left, jnp.where(left == z - 1, n, left), z - 1).start()

            return carry

        lax.fori_loop(0, n - 1, step, 0)

    def piece(s, p, to):
        return pltpu.make_async_remote_copy(
            src_ref=pb.at[s, p], dst_ref=rp.at[s, g], send_sem=ps.at[s, p],
            recv_sem=pr.at[s, g], device_id=(to, z), device_id_type=MESH,
        )

    def piece_from(s, p):
        return pltpu.make_async_remote_copy(
            src_ref=pb.at[s, 0], dst_ref=rp.at[s, p], send_sem=ps.at[s, 0],
            recv_sem=pr.at[s, p], device_id=(mate, z), device_id_type=MESH,
        )

    def inner(s):
        acc[pl.ds(0, R), :] = term(z, s)

        @pl.when(z > 0)
        def _():
            move(s, z, z, other_z).wait_recv()
            acc[pl.ds(0, R), :] += rb[s, z].astype(f32)

        @pl.when(z < n - 1)
        def _():
            move(s, z, n, other_z).wait_recv()
            acc[pl.ds(0, R), :] += rb[s, n].astype(f32)

        def tile(i, carry):
            at = pl.multiple_of(i * TILE, TILE)
            place = pl.ds(pl.multiple_of(s * R + i * TILE, TILE), TILE)
            gradient = acc[pl.ds(at, TILE), :]
            codes = q[place, :]
            first_code = (codes >> 4).astype(f32)
            second_code = (codes & 15).astype(f32)
            first_old = jnp.minimum(fcol[place, :], fcm[...]) * ((first_code - 7.5) / 7.5)
            level = (second_code + 1.0) * (1.0 / 16.0)
            second_old = jnp.minimum(scol[place, :], scm[...]) * (level * level)
            first_new = beta_one * first_old + (1.0 - beta_one) * gradient
            second_new = beta_two * second_old + (1.0 - beta_two) * gradient * gradient
            fn[place, :] = first_new
            sn[place, :] = second_new
            update = (first_new / bias_one) / (jnp.sqrt(second_new / bias_two) + adam_eps)
            pseudo = inner_rate * (update + weight_decay * w[place, :].astype(f32))
            pb[s, i // (PR // TILE), pl.ds(lax.rem(i, PR // TILE) * TILE, TILE), :] = pseudo.astype(bf16)
            size = jnp.abs(first_new)
            ca[...] = jnp.maximum(ca[...], size)
            cb[...] = jnp.maximum(cb[...], second_new)
            frn[place, :] = jnp.max(size, axis=1, keepdims=True) + stat_eps
            srn[place, :] = jnp.max(second_new, axis=1, keepdims=True) + stat_eps
            return carry

        lax.fori_loop(0, R // TILE, tile, 0)

        def send(d, carry):
            p = lax.rem(g + d, G)

            @pl.when(p < NP)
            def _():
                piece(s, p, p).start()

            return carry

        lax.fori_loop(1, G, send, 0)

    def share(s, p, to):
        own = pl.ds(pl.multiple_of(p * PR, PR), PR)
        return pltpu.make_async_remote_copy(
            src_ref=av.at[s, own], dst_ref=av.at[s, own], send_sem=as_.at[s, to],
            recv_sem=ar.at[s, p], device_id=(to, z), device_id_type=MESH,
        )

    def reduce(s):
        @pl.when(g < NP)
        def _():
            acc[pl.ds(0, PR), :] = pb[s, g].astype(f32)

            def add(d, carry):
                p = lax.rem(g + d, G)
                piece_from(s, p).wait_recv()
                acc[pl.ds(0, PR), :] += rp[s, p].astype(f32)
                return carry

            lax.fori_loop(1, G, add, 0)
            av[s, pl.ds(pl.multiple_of(g * PR, PR), PR), :] = (
                acc[pl.ds(0, PR), :] * (1.0 / G)
            ).astype(bf16)

            def send(d, carry):
                share(s, g, lax.rem(g + d, G)).start()
                return carry

            lax.fori_loop(1, G, send, 0)

    def relay(s, c, way, to):
        part = pl.ds(pl.multiple_of(s * R + h * half, half), half)
        return pltpu.make_async_remote_copy(
            src_ref=wf.at[c, part], dst_ref=wf.at[c, part], send_sem=gs.at[way, s, c],
            recv_sem=gr.at[s, c], device_id=(g, to), device_id_type=MESH,
        )

    def hand(s, c):
        part = pl.ds(pl.multiple_of(s * R + h * half, half), half)
        return pltpu.make_async_remote_copy(
            src_ref=wf.at[c, part], dst_ref=wf.at[c, part], send_sem=hs.at[s, c],
            recv_sem=hr.at[s, c], device_id=(mate, z), device_id_type=MESH,
        )

    def hand_from(s, c):
        part = pl.ds(pl.multiple_of(s * R + (1 - h) * half, half), half)
        return pltpu.make_async_remote_copy(
            src_ref=wf.at[c, part], dst_ref=wf.at[c, part], send_sem=hs.at[s, c],
            recv_sem=hr.at[s, c], device_id=(mate, z), device_id_type=MESH,
        )

    def outer(s):
        def wait(p, carry):
            @pl.when(p != g)
            def _():
                share(s, p, mate).wait_recv()

            return carry

        lax.fori_loop(0, NP, wait, 0)

        def tile(i, carry):
            place = pl.ds(pl.multiple_of(s * R + i * TILE, TILE), TILE)
            sent = av[s, pl.ds(pl.multiple_of(i * TILE, TILE), TILE), :]
            o_a[place, :] = sent
            averaged = sent.astype(f32)
            momentum = outer_beta * m[place, :] + averaged
            fresh = w[place, :].astype(f32) - outer_rate * (averaged + outer_beta * momentum)
            wf[z, place, :] = fresh.astype(bf16)
            return carry

        lax.fori_loop(0, R // TILE, tile, 0)

        @pl.when(z < n - 1)
        def _():
            relay(s, z, 0, z + 1).start()

        @pl.when(z > 0)
        def _():
            relay(s, z, 1, z - 1).start()

    def hop(s, j):
        @pl.when(z - j >= 0)
        def _():
            c = z - j
            relay(s, c, 0, other_z).wait_recv()

            @pl.when(z < n - 1)
            def _():
                relay(s, c, 0, z + 1).start()

            hand(s, c).start()

        @pl.when(z + j < n)
        def _():
            c = z + j
            relay(s, c, 1, other_z).wait_recv()

            @pl.when(z > 0)
            def _():
                relay(s, c, 1, z - 1).start()

            hand(s, c).start()

    def hops(u):
        for j in range(1, n):
            if (u - 3 - j) % 2 == 0 and 0 <= (u - 3 - j) // 2 < S:
                hop((u - 3 - j) // 2, j)

    @pl.when((z == 0) | (z == n - 1))
    def _():
        def every(s, carry):
            stream(s)
            return carry

        lax.fori_loop(0, S, every, 0)

    for load in loads[2:]:
        load.wait()

    def column_max(slot, to):
        return pltpu.make_async_remote_copy(
            src_ref=cmb.at[z], dst_ref=cmb.at[z], send_sem=cs.at[slot],
            recv_sem=cr.at[z], device_id=(g, to), device_id_type=MESH,
        )

    def column_max_from(c):
        return pltpu.make_async_remote_copy(
            src_ref=cmb.at[c], dst_ref=cmb.at[c], send_sem=cs.at[0],
            recv_sem=cr.at[c], device_id=(g, other_z), device_id_type=MESH,
        )

    for s in range(S + 1):
        if s < S:
            @pl.when((z > 0) & (z < n - 1))
            def _():
                stream(s)
        hops(2 * s)
        if s >= 1:
            reduce(s - 1)
        if s < S:
            inner(s)
        if s == S - 1:
            cmb[z, pl.ds(0, 1), :] = jnp.max(ca[...], axis=0, keepdims=True)
            cmb[z, pl.ds(1, 1), :] = jnp.max(cb[...], axis=0, keepdims=True)
            for d in range(1, n):
                column_max(d, lax.rem(z + d, n)).start()
        if s >= 1:
            outer(s - 1)
        hops(2 * s + 1)

    for d in range(1, n):
        column_max_from(lax.rem(z + d, n)).wait_recv()
    scales = jnp.max(cmb[...], axis=0) + stat_eps
    o_fcm[...] = scales[0:1]
    o_scm[...] = scales[1:2]

    def states(s):
        def tile(i, carry):
            place = pl.ds(pl.multiple_of(s * R + i * TILE, TILE), TILE)
            o_fs[place, :] = (fn[place, :] / jnp.minimum(frn[place, :], o_fcm[...])).astype(bf16)
            o_ss[place, :] = (sn[place, :] / jnp.minimum(srn[place, :], o_scm[...])).astype(bf16)
            return carry

        lax.fori_loop(0, R // TILE, tile, 0)
        block = pl.ds(s * R, R)
        o_frm[:, block] = to_row(frn[block, :])
        o_srm[:, block] = to_row(srn[block, :])

    for s in range(S):
        states(s)

    def product(c):
        columns = pl.ds(pl.multiple_of(c * rows, 128), rows)
        return jnp.dot(x[:, columns], wf[c], preferred_element_type=f32)

    acc[...] = product(z)
    for u in range(2 * S + 2, 2 * S + 2 + n - 1):
        hops(u)

    def gather(j, carry):
        for c in (z - j, z + j):
            @pl.when((c >= 0) & (c < n))
            def _():
                for s in range(S):
                    hand_from(s, c).wait_recv()
                acc[...] += product(c)
        return carry

    lax.fori_loop(1, n, gather, 0)
    o_k[...] = acc[...].astype(bf16)

    for s in range(S):
        def sent(c, carry):
            @pl.when(c != z)
            def _():
                move(s, c, c, other_z).wait_send()
                hand(s, c).wait_send()

            @pl.when((c <= z) & (z < n - 1))
            def _():
                relay(s, c, 0, other_z).wait_send()

            @pl.when((c >= z) & (z > 0))
            def _():
                relay(s, c, 1, other_z).wait_send()

            return carry

        lax.fori_loop(0, n, sent, 0)

        def plane(p, carry):
            @pl.when(p != g)
            def _():
                @pl.when(p < NP)
                def _():
                    piece(s, p, mate).wait_send()

                @pl.when(g < NP)
                def _():
                    share(s, g, p).wait_send()

            return carry

        lax.fori_loop(0, G, plane, 0)
    for d in range(1, n):
        column_max(d, other_z).wait_send()


def finish(avg, w, m, *refs):
    o_w, o_m = refs[7:9]
    averaged = avg[...].astype(f32)
    momentum = outer_beta * m[...] + averaged
    o_m[...] = momentum
    o_w[...] = w[...].astype(f32) - outer_rate * (averaged + outer_beta * momentum)
    for src, dst in zip(refs[:7], refs[9:]):
        dst[...] = src[...]


def local(x, ct, w, m, q, frm, fcm, srm, scm):
    n, G = lax.axis_size("fsdp"), lax.axis_size("grp")
    rows, C = w.shape
    T, K = x.shape[1:]
    R = min(128, rows)
    S = rows // R
    PR = max(TILE, R // G)
    NP = R // PR
    hbm = pl.BlockSpec(memory_space=pl.ANY)
    vmem = pl.BlockSpec(memory_space=pltpu.VMEM)
    dma = pltpu.SemaphoreType.DMA
    shape = jax.ShapeDtypeStruct
    outs = pl.pallas_call(
        functools.partial(kernel, n, G, S, R, PR, NP),
        out_shape=(
            shape((rows, C), bf16), shape((rows, C), bf16), shape((rows, C), bf16),
            shape((1, rows), f32), shape((1, C), f32),
            shape((1, rows), f32), shape((1, C), f32),
            shape((T, C), bf16),
        ),
        in_specs=[hbm] * 5 + [vmem] * 4,
        out_specs=(vmem,) * 8,
        scratch_shapes=[
            pltpu.VMEM((T, K), bf16), pltpu.VMEM((T, C), bf16), pltpu.VMEM((rows, C), bf16),
            pltpu.VMEM((rows, C), f32), pltpu.VMEM((rows, C), jnp.int32),
            pltpu.VMEM((S, n, R, C), bf16), pltpu.VMEM((S, n + 1, R, C), bf16),
            pltpu.VMEM((S, NP, PR, C), bf16), pltpu.VMEM((S, G, PR, C), bf16),
            pltpu.VMEM((S, R, C), bf16), pltpu.VMEM((n, rows, C), bf16),
            pltpu.VMEM((rows, C), f32), pltpu.VMEM((rows, C), f32), pltpu.VMEM((T, C), f32),
            pltpu.VMEM((rows, 1), f32), pltpu.VMEM((rows, 1), f32),
            pltpu.VMEM((rows, 1), f32), pltpu.VMEM((rows, 1), f32),
            pltpu.VMEM((TILE, C), f32), pltpu.VMEM((TILE, C), f32), pltpu.VMEM((n, 2, C), f32),
            dma((5,)), dma((S, n)), dma((S, n + 1)), dma((S, NP)), dma((S, G)),
            dma((S, G)), dma((S, NP)), dma((2, S, n)), dma((S, n)), dma((S, n)), dma((S, n)),
            dma((n,)), dma((n,)),
        ],
        compiler_params=pltpu.CompilerParams(
            collective_id=0, has_side_effects=True, vmem_limit_bytes=60 * 1024 * 1024
        ),
    )(x[0], ct[0], w, m, q[0], frm, fcm, srm, scm)
    avg, fs, ss, nfr, nfc, nsr, nsc, keys = outs
    steps = 4
    high = pl.BlockSpec((rows // steps, C), lambda i: (i, 0))
    tall = pl.BlockSpec((T // steps, C), lambda i: (i, 0))
    wide = pl.BlockSpec((1, rows), lambda i: (0, 0))
    flat = pl.BlockSpec((1, C), lambda i: (0, 0))
    blocks = (high, high, tall, wide, flat, wide, flat)
    new_w, new_m, fs, ss, keys, nfr, nfc, nsr, nsc = pl.pallas_call(
        finish,
        grid=(steps,),
        out_shape=(
            shape((rows, C), f32), shape((rows, C), f32),
            shape((rows, C), bf16), shape((rows, C), bf16), shape((T, C), bf16),
            shape((1, rows), f32), shape((1, C), f32),
            shape((1, rows), f32), shape((1, C), f32),
        ),
        in_specs=(high,) * 3 + blocks,
        out_specs=(high,) * 2 + blocks,
    )(avg, w, m, fs, ss, keys, nfr, nfc, nsr, nsc)
    return new_w, new_m, fs[None], ss[None], nfr, nfc, nsr, nsc, keys[None]


def solution(mesh):
    return jax.shard_map(
        local,
        mesh=mesh,
        in_specs=(
            P("grp", "fsdp", None), P("grp", "fsdp", None), P("fsdp", None), P("fsdp", None),
            P("grp", "fsdp", None), P("grp", "fsdp"), P("grp", None), P("grp", "fsdp"),
            P("grp", None),
        ),
        out_specs=(
            P("fsdp", None), P("fsdp", None), P("grp", "fsdp", None), P("grp", "fsdp", None),
            P("grp", "fsdp"), P("grp", None), P("grp", "fsdp"), P("grp", None),
            P("grp", "fsdp", None),
        ),
        check_vma=False,
    )
```

profile of v0, /device:TPU:1, one launch (start us, length us, event | category | flops | bytes accessed | tf_op | source)
XLA Modules:
  0.0 121.7 jit_solution(7599327422034823915)
XLA Ops:
  0.6 115.5 %shard_map.160 = (bf16[512,768]{1,0:T(8,128)(2,1)}, bf16[512,768]{1,0:T(8,128)(2,1)}, bf16[512,768]{1,0:T(8,128)(2,1)}, f32[1,512]{1,0:T(1,128)}, f32[1,768]{1,0...) custom-call(bf16[512,2048]{1,0:T(8,128)(2,1)} %bitcast.6, bf16[512,768]{1,0:T(8,128)(2,1)} %bitcast.8, ...), custom_call_target="tpu_custom_call" | custom-call | tf_op jit(solution)/shard_map/pallas_call | solution.py:440
  116.1 5.6 %shard_map.161 = (f32[512,768]{1,0:T(8,128)}, f32[512,768]{1,0:T(8,128)}, bf16[512,768]{1,0:T(8,128)(2,1)}, bf16[512,768]{1,0:T(8,128)(2,1)}, bf16[512,768]{1,0:...) custom-call(bf16[512,768]{1,0:T(8,128)(2,1)} %get-tuple-element.26.avg, ...), custom_call_target="tpu_custom_call" | custom-call | tf_op jit(solution)/shard_map/pallas_call | solution.py:475
where the time goes:
time: 122 us
  Pallas kernels  121 us (99%)
    pallas_call x1, Pallas kernels, local(): pl.pallas_call(functools.partial(kernel, n, G, S, R, PR, NP), out_shape=(...  115 us
    pallas_call x1, Pallas kernels, local(): pl.pallas_call(finish, grid=(steps,), out_shape=(shape((rows, C), f32), s...  5.57 us

commit v1 on v0

v1 whole, which is shorter than its diff:
```python
import functools
import typing
import jax
import jax.numpy as jnp
from jax import lax
from jax.experimental import pallas as pl
from jax.experimental.pallas import tpu as pltpu
from jax.sharding import PartitionSpec as P

MESH = pl.DeviceIdType.MESH
f32, bf16 = jnp.float32, jnp.bfloat16
beta_one = 0.9
beta_two = 0.95
bias_one = 1.0 - 0.9**10
bias_two = 1.0 - 0.95**10
adam_eps = 1e-08
inner_rate = 0.01
weight_decay = 0.1
outer_rate = 0.7
outer_beta = 0.9
stat_eps = 1e-06
TILE = 16
UNIT = 128


class Stage(typing.NamedTuple):
    o: int
    R: int
    PR: int
    PC: int
    nc: int
    NP: int


def plan(rows, C, G):
    sizes = [UNIT] * (rows // UNIT - 1) + [UNIT // 2] * 2
    stages, o = [], 0
    for R in sizes:
        PR = max(TILE, R // G)
        nc = max(k for k in (1, 2, 3, 6) if k == 1 or (R // PR * k <= G and C % (128 * k) == 0))
        stages.append(Stage(o, R, PR, C // nc, nc, R // PR * nc))
        o += R
    return stages


def to_column(row):
    return jnp.broadcast_to(row, (128, row.shape[1])).T[:, :1]


def to_row(column):
    return jnp.broadcast_to(column, (column.shape[0], 128)).T[:1, :]


def kernel(
    n, G, stages,
    x_hbm, c_hbm, w_hbm, m_hbm, q_hbm, frm_hbm, fcm_hbm, srm_hbm, scm_hbm,
    o_w, o_m, o_fs, o_ss, o_frm, o_fcm, o_srm, o_scm, o_k,
    x, ct, w, m, q, frm, fcm, srm, scm,
    tb, rb, pb, rp, av, wf, fn, sn, acc, keys, fcol, scol, frn, srn, ca, cb, cmb,
    ld, ts, tr, ps, pr, as_, ar, gs, gr, ds, hs, hr, cs, cr,
):
    g = lax.axis_index("grp")
    z = lax.axis_index("fsdp")
    S = len(stages)
    rows, C = w.shape
    h = lax.rem(g, 2)
    mate = g + 1 - 2 * h
    other_z = lax.rem(z + 1, n)
    cut = rows - UNIT

    loads = [
        pltpu.make_async_copy(src, dst, ld.at[i])
        for i, (src, dst) in enumerate((
            (c_hbm, ct), (x_hbm, x), (frm_hbm, frm), (fcm_hbm, fcm), (srm_hbm, srm),
            (scm_hbm, scm), (q_hbm, q), (w_hbm, w), (m_hbm, m),
        ))
    ]
    barrier = pltpu.get_barrier_semaphore()
    for d in range(1, n):
        pl.semaphore_signal(
            barrier, inc=1, device_id=(g, lax.rem(z + d, n)), device_id_type=MESH
        )
    for d in range(1, G):
        pl.semaphore_signal(
            barrier, inc=1, device_id=(lax.rem(g + d, G), z), device_id_type=MESH
        )
    for load in loads:
        load.start()
    ca[...] = jnp.zeros_like(ca)
    cb[...] = jnp.zeros_like(cb)
    loads[0].wait()
    loads[1].wait()
    with jax.named_scope("barrier"):
        pl.semaphore_wait(barrier, G - 1 + n - 1)

    def term(c, s):
        st = stages[s]
        lead = st.o % UNIT
        columns = pl.ds(pl.multiple_of(c * rows + (st.o - lead), UNIT), UNIT)
        whole = lax.dot_general(
            x[:, columns], ct[...], (((0,), (0,)), ((), ())), preferred_element_type=f32
        )
        return whole[lead : lead + st.R]

    def block(s):
        return pl.ds(stages[s].o, stages[s].R)

    def move(s, c, slot, to):
        return pltpu.make_async_remote_copy(
            src_ref=tb.at[c, block(s)], dst_ref=rb.at[slot, block(s)], send_sem=ts.at[s, c],
            recv_sem=tr.at[s, slot], device_id=(g, to), device_id_type=MESH,
        )

    def stream(s):
        R = stages[s].R
        low = 2 * z < n

        def step(k, carry):
            nr = n - 1 - z
            right = jnp.where(low, jnp.where(k < nr, 1, 0), jnp.where(k < z, 0, 1)) == 1
            c = jnp.where(
                low, jnp.where(k < nr, n - 1 - k, k - nr), jnp.where(k < z, k, n - 1 - k + z)
            )
            to = jnp.where(right, z + 1, z - 1)
            slot = jnp.where(jnp.where(right, -1, z - 1) == c, n, c)
            acc[pl.ds(0, R), :] = term(c, s)

            @pl.when(jnp.where(right, z, n - 1 - z) == 0)
            def _():
                tb[c, block(s), :] = acc[pl.ds(0, R), :].astype(bf16)

            @pl.when(jnp.where(right, z, n - 1 - z) > 0)
            def _():
                move(s, c, c, other_z).wait_recv()
                tb[c, block(s), :] = (acc[pl.ds(0, R), :] + rb[c, block(s), :].astype(f32)).astype(bf16)

            move(s, c, slot, to).start()
            return carry

        lax.fori_loop(0, n - 1, step, 0)

    def place_of(s, p):
        st = stages[s]
        return (
            pl.ds(pl.multiple_of(st.o + p // st.nc * st.PR, TILE), st.PR),
            pl.ds(pl.multiple_of(lax.rem(p, st.nc) * st.PC, 128), st.PC),
        )

    def piece(s, p, to):
        st = stages[s]
        return pltpu.make_async_remote_copy(
            src_ref=pb.at[place_of(s, p)],
            dst_ref=rp.at[s, g, pl.ds(0, st.PR), pl.ds(0, st.PC)], send_sem=ps.at[s, p],
            recv_sem=pr.at[s, g], device_id=(to, z), device_id_type=MESH,
        )

    def piece_from(s, p):
        st = stages[s]
        here = rp.at[s, p, pl.ds(0, st.PR), pl.ds(0, st.PC)]
        return pltpu.make_async_remote_copy(
            src_ref=here, dst_ref=here, send_sem=ps.at[s, 0],
            recv_sem=pr.at[s, p], device_id=(mate, z), device_id_type=MESH,
        )

    def inner(s):
        st = stages[s]
        R = st.R
        acc[pl.ds(0, R), :] = term(z, s)

        @pl.when(z > 0)
        def _():
            move(s, z, z, other_z).wait_recv()
            acc[pl.ds(0, R), :] += rb[z, block(s), :].astype(f32)

        @pl.when(z < n - 1)
        def _():
            move(s, z, n, other_z).wait_recv()
            acc[pl.ds(0, R), :] += rb[n, block(s), :].astype(f32)

        def tile(i, carry):
            at = pl.multiple_of(i * TILE, TILE)
            place = pl.ds(pl.multiple_of(st.o + i * TILE, TILE), TILE)
            gradient = acc[pl.ds(at, TILE), :]
            codes = q[place, :]
            first_code = (codes >> 4).astype(f32)
            second_code = (codes & 15).astype(f32)
            second_code = second_code + 1.0
            first_new = (
                jnp.minimum(fcol[place, :], fcm[...]) * (first_code - 7.5)
                + (1.0 - beta_one) * gradient
            )
            second_new = (
                jnp.minimum(scol[place, :], scm[...]) * (second_code * second_code)
                + (1.0 - beta_two) * gradient * gradient
            )
            fn[place, :] = first_new
            sn[place, :] = second_new
            update = (first_new * (inner_rate / bias_one)) / (
                jnp.sqrt(second_new * (1.0 / bias_two)) + adam_eps
            )
            pseudo = update + (inner_rate * weight_decay) * w[place, :].astype(f32)
            pb[place, :] = pseudo.astype(bf16)
            size = jnp.abs(first_new)
            ca[...] = jnp.maximum(ca[...], size)
            cb[...] = jnp.maximum(cb[...], second_new)
            frn[place, :] = jnp.max(size, axis=1, keepdims=True) + stat_eps
            srn[place, :] = jnp.max(second_new, axis=1, keepdims=True) + stat_eps
            return carry

        lax.fori_loop(0, R // TILE, tile, 0)

        def send(d, carry):
            p = lax.rem(g + d, G)

            @pl.when(p < st.NP)
            def _():
                piece(s, p, p).start()

            return carry

        lax.fori_loop(1, G, send, 0)

    def share(s, p, to):
        return pltpu.make_async_remote_copy(
            src_ref=av.at[place_of(s, p)], dst_ref=av.at[place_of(s, p)], send_sem=as_.at[s, to],
            recv_sem=ar.at[s, p], device_id=(to, z), device_id_type=MESH,
        )

    def reduce(s):
        st = stages[s]
        top = (pl.ds(0, st.PR), pl.ds(0, st.PC))

        @pl.when(g < st.NP)
        def _():
            acc[top] = pb[place_of(s, g)].astype(f32)

            def add(d, carry):
                p = lax.rem(g + d, G)
                piece_from(s, p).wait_recv()
                acc[top] += rp[(s, p) + top].astype(f32)
                return carry

            lax.fori_loop(1, G, add, 0)
            av[place_of(s, g)] = (acc[top] * (1.0 / G)).astype(bf16)

            def send(d, carry):
                share(s, g, lax.rem(g + d, G)).start()
                return carry

            lax.fori_loop(1, G, send, 0)

    def half(s, which):
        st = stages[s]
        return pl.ds(pl.multiple_of(st.o + which * (st.R // 2), TILE), st.R // 2)

    def relay(s, c, way, to):
        part = half(s, h)
        return pltpu.make_async_remote_copy(
            src_ref=wf.at[c, part], dst_ref=wf.at[c, part], send_sem=gs.at[way, s, c],
            recv_sem=gr.at[s, c], device_id=(g, to), device_id_type=MESH,
        )

    def direct(to):
        part = half(S - 1, h)
        return pltpu.make_async_remote_copy(
            src_ref=wf.at[z, part], dst_ref=wf.at[z, part], send_sem=ds.at[to],
            recv_sem=gr.at[S - 1, z], device_id=(g, to), device_id_type=MESH,
        )

    def hand(s, c):
        part = half(s, h)
        return pltpu.make_async_remote_copy(
            src_ref=wf.at[c, part], dst_ref=wf.at[c, part], send_sem=hs.at[s, c],
            recv_sem=hr.at[s, c], device_id=(mate, z), device_id_type=MESH,
        )

    def hand_from(s, c):
        part = half(s, 1 - h)
        return pltpu.make_async_remote_copy(
            src_ref=wf.at[c, part], dst_ref=wf.at[c, part], send_sem=hs.at[s, c],
            recv_sem=hr.at[s, c], device_id=(mate, z), device_id_type=MESH,
        )

    def outer(s):
        st = stages[s]

        def wait(p, carry):
            @pl.when(p != g)
            def _():
                share(s, p, mate).wait_recv()

            return carry

        lax.fori_loop(0, st.NP, wait, 0)

        def tile(i, carry):
            place = pl.ds(pl.multiple_of(st.o + i * TILE, TILE), TILE)
            averaged = av[place, :].astype(f32)
            momentum = outer_beta * m[place, :] + averaged
            fresh = w[place, :].astype(f32) - outer_rate * (averaged + outer_beta * momentum)
            o_m[place, :] = momentum
            o_w[place, :] = fresh
            wf[z, place, :] = fresh.astype(bf16)
            return carry

        lax.fori_loop(0, st.R // TILE, tile, 0)
        if s < S - 1:
            @pl.when(z < n - 1)
            def _():
                relay(s, z, 0, z + 1).start()

            @pl.when(z > 0)
            def _():
                relay(s, z, 1, z - 1).start()
        else:
            for d in range(1, n):
                direct(lax.rem(z + d, n)).start()

    def from_left(s, c):
        relay(s, c, 0, other_z).wait_recv()

        @pl.when(z < n - 1)
        def _():
            relay(s, c, 0, z + 1).start()

        hand(s, c).start()

    def from_right(s, c):
        relay(s, c, 1, other_z).wait_recv()

        @pl.when(z > 0)
        def _():
            relay(s, c, 1, z - 1).start()

        hand(s, c).start()

    def hop_mid(s, j):
        @pl.when(z - j >= 1)
        def _():
            from_left(s, z - j)

        @pl.when(z + j <= n - 2)
        def _():
            from_right(s, z + j)

    def hop_end(s, j):
        @pl.when(z == j)
        def _():
            from_left(s, z - j)

        @pl.when(z == n - 1 - j)
        def _():
            from_right(s, z + j)

    @pl.when((z == 0) | (z == n - 1))
    def _():
        for s in range(S):
            with jax.named_scope(f"end{s}"):
                stream(s)

    for load in loads[2:]:
        load.wait()
    fcm[...] = fcm[...] * (beta_one / 7.5)
    scm[...] = scm[...] * (beta_two / 256.0)
    for o in range(0, rows, UNIT):
        part = pl.ds(o, UNIT)
        fcol[part, :] = to_column(frm[:, part] * (beta_one / 7.5))
        scol[part, :] = to_column(srm[:, part] * (beta_two / 256.0))

    def column_max(slot, to):
        return pltpu.make_async_remote_copy(
            src_ref=cmb.at[z], dst_ref=cmb.at[z], send_sem=cs.at[slot],
            recv_sem=cr.at[z], device_id=(g, to), device_id_type=MESH,
        )

    def column_max_from(c):
        return pltpu.make_async_remote_copy(
            src_ref=cmb.at[c], dst_ref=cmb.at[c], send_sem=cs.at[0],
            recv_sem=cr.at[c], device_id=(g, other_z), device_id_type=MESH,
        )

    done_mid = set()
    for s in range(S):
        @pl.when((z > 0) & (z < n - 1))
        def _():
            with jax.named_scope(f"stream{s}"):
                stream(s)
        if s >= 1:
            with jax.named_scope(f"reduce{s-1}"):
                reduce(s - 1)
        with jax.named_scope(f"inner{s}"):
            inner(s)
        if s == S - 1:
            cmb[z, pl.ds(0, 1), :] = jnp.max(ca[...], axis=0, keepdims=True)
            cmb[z, pl.ds(1, 1), :] = jnp.max(cb[...], axis=0, keepdims=True)
            for d in range(1, n):
                column_max(d, lax.rem(z + d, n)).start()
        if s >= 1:
            with jax.named_scope(f"outer{s-1}"):
                outer(s - 1)
        for t in range(S - 1):
            for j in range(1, n):
                if t + 1 + j == s:
                    done_mid.add((t, j))
                    with jax.named_scope(f"mid{t}{j}"):
                        hop_mid(t, j)

    def states():
        for c in range(1, n):
            column_max_from(lax.rem(z + c, n)).wait_recv()
        scales = jnp.max(cmb[...], axis=0) + stat_eps
        o_fcm[...] = scales[0:1]
        o_scm[...] = scales[1:2]
        fcm[...] = 1.0 / o_fcm[...]
        scm[...] = 1.0 / o_scm[...]

        def tile(i, carry):
            place = pl.ds(pl.multiple_of(i * TILE, TILE), TILE)
            first_inverse = jnp.maximum(1.0 / frn[place, :], fcm[...])
            second_inverse = jnp.maximum(1.0 / srn[place, :], scm[...])
            o_fs[place, :] = (fn[place, :] * first_inverse).astype(bf16)
            o_ss[place, :] = (sn[place, :] * second_inverse).astype(bf16)
            return carry

        lax.fori_loop(0, rows // TILE, tile, 0)
        for o in range(0, rows, UNIT):
            part = pl.ds(o, UNIT)
            o_frm[:, part] = to_row(frn[part, :])
            o_srm[:, part] = to_row(srn[part, :])

    def product(c, o, width):
        columns = pl.ds(pl.multiple_of(c * rows + o, UNIT), width)
        return jnp.dot(x[:, columns], wf[c, pl.ds(o, width), :], preferred_element_type=f32)

    def others(body):
        def step(j, carry):
            for c in (z - j, z + j):
                @pl.when((c >= 0) & (c < n))
                def _():
                    body(c)

            return carry

        lax.fori_loop(1, n, step, 0)

    def gather_early(c):
        for s in range(S - 2):
            hand_from(s, c).wait_recv()
        keys[...] += product(c, 0, cut)

    def own():
        if cut:
            keys[...] = product(z, 0, cut)
            keys[...] += product(z, cut, UNIT)
        else:
            keys[...] = product(z, cut, UNIT)

    todo = [(7.0, "reduce", functools.partial(reduce, S - 1)), (11.0, "outer", functools.partial(outer, S - 1))]
    todo += [(11.1, "own", own), (12.6, "states", states)]
    if cut:
        todo += [(14.5, "early", None)]
    for s in range(S - 1):
        for j in range(1, n):
            if (s, j) not in done_mid:
                when = 4.0 * j + 4.0 if s == S - 2 else 0.0
                todo.append((when, f"mid{s}{j}", functools.partial(hop_mid, s, j)))
            when = 1.7 + 2.1 * (s + 1) + 3.8 * (j - 1)
            todo.append((when, f"hop{s}{j}", functools.partial(hop_end, s, j)))
    late = [t for t in todo if t[1].startswith("hop") and t[0] > 13.0]
    for _, name, run in sorted((t for t in todo if t not in late), key=lambda t: t[0]):
        if name == "early":
            for _, lname, lrun in sorted(late, key=lambda t: t[0]):
                with jax.named_scope(lname):
                    lrun()
            with jax.named_scope("early"):
                others(gather_early)
        else:
            with jax.named_scope(name):
                run()
    if not cut:
        for _, _, run in sorted(late, key=lambda t: t[0]):
            run()

    def finish_from(c):
        part = half(S - 1, h)
        pltpu.make_async_remote_copy(
            src_ref=wf.at[c, part], dst_ref=wf.at[c, part], send_sem=ds.at[0],
            recv_sem=gr.at[S - 1, c], device_id=(g, other_z), device_id_type=MESH,
        ).wait_recv()
        hand(S - 1, c).start()

    with jax.named_scope("lastrecv"):
        others(finish_from)

    def gather_last(c):
        for s in (S - 2, S - 1):
            hand_from(s, c).wait_recv()
        keys[...] += product(c, cut, UNIT)

    with jax.named_scope("gatherlast"):
        others(gather_last)
    with jax.named_scope("okeys"):
        o_k[...] = keys[...].astype(bf16)

    with jax.named_scope("sends"):
        for s in range(S):
            def chunk(c, carry):
                @pl.when(c != z)
                def _():
                    move(s, c, c, other_z).wait_send()
                    hand(s, c).wait_send()

                if s < S - 1:
                    @pl.when((c <= z) & (z < n - 1))
                    def _():
                        relay(s, c, 0, other_z).wait_send()

                    @pl.when((c >= z) & (z > 0))
                    def _():
                        relay(s, c, 1, other_z).wait_send()

                return carry

            lax.fori_loop(0, n, chunk, 0)

            def plane(p, carry):
                @pl.when((p != g) & (p < stages[s].NP))
                def _():
                    piece(s, p, mate).wait_send()

                @pl.when((p != g) & (g < stages[s].NP))
                def _():
                    share(s, g, p).wait_send()

                return carry

            lax.fori_loop(0, G, plane, 0)
        for d in range(1, n):
            direct(lax.rem(z + d, n)).wait_send()
            column_max(d, other_z).wait_send()


def finish(*refs):
    k = (len(refs) - 1) // 2
    sems = refs[-1]
    copies = [
        pltpu.make_async_copy(src, dst, sems.at[i])
        for i, (src, dst) in enumerate(zip(refs[:k], refs[k:-1]))
    ]
    for copy in copies:
        copy.start()
    for copy in copies:
        copy.wait()


def local(x, ct, w, m, q, frm, fcm, srm, scm):
    n, G = lax.axis_size("fsdp"), lax.axis_size("grp")
    rows, C = w.shape
    T, K = x.shape[1:]
    stages = plan(rows, C, G)
    S = len(stages)
    PR = max(st.PR for st in stages)
    hbm = pl.BlockSpec(memory_space=pltpu.HBM)
    vmem = pl.BlockSpec(memory_space=pltpu.VMEM)
    dma = pltpu.SemaphoreType.DMA
    shape = jax.ShapeDtypeStruct
    outs = pl.pallas_call(
        functools.partial(kernel, n, G, stages),
        out_shape=(
            pltpu.VMEM((rows, C), f32), pltpu.VMEM((rows, C), f32),
            pltpu.VMEM((rows, C), bf16), pltpu.VMEM((rows, C), bf16),
            pltpu.VMEM((1, rows), f32), pltpu.VMEM((1, C), f32),
            pltpu.VMEM((1, rows), f32), pltpu.VMEM((1, C), f32),
            pltpu.VMEM((T, C), bf16),
        ),
        in_specs=[hbm] * 9,
        out_specs=(vmem,) * 9,
        scratch_shapes=[
            pltpu.VMEM((T, K), bf16), pltpu.VMEM((T, C), bf16), pltpu.VMEM((rows, C), bf16),
            pltpu.VMEM((rows, C), f32), pltpu.VMEM((rows, C), jnp.int32),
            pltpu.VMEM((1, rows), f32), pltpu.VMEM((1, C), f32),
            pltpu.VMEM((1, rows), f32), pltpu.VMEM((1, C), f32),
            pltpu.VMEM((n, rows, C), bf16), pltpu.VMEM((n + 1, rows, C), bf16),
            pltpu.VMEM((rows, C), bf16), pltpu.VMEM((S, G, PR, C), bf16),
            pltpu.VMEM((rows, C), bf16), pltpu.VMEM((n, rows, C), bf16),
            pltpu.VMEM((rows, C), f32), pltpu.VMEM((rows, C), f32),
            pltpu.VMEM((UNIT, C), f32), pltpu.VMEM((T, C), f32),
            pltpu.VMEM((rows, 1), f32), pltpu.VMEM((rows, 1), f32),
            pltpu.VMEM((rows, 1), f32), pltpu.VMEM((rows, 1), f32),
            pltpu.VMEM((TILE, C), f32), pltpu.VMEM((TILE, C), f32), pltpu.VMEM((n, 2, C), f32),
            dma((9,)), dma((S, n)), dma((S, n + 1)), dma((S, G)), dma((S, G)),
            dma((S, G)), dma((S, G)), dma((2, S, n)), dma((S, n)), dma((n,)),
            dma((S, n)), dma((S, n)), dma((n,)), dma((n,)),
        ],
        compiler_params=pltpu.CompilerParams(
            collective_id=0, has_side_effects=True, vmem_limit_bytes=54 * 1024 * 1024
        ),
    )(x[0], ct[0], w, m, q[0], frm, fcm, srm, scm)
    done = pl.pallas_call(
        finish,
        out_shape=tuple(shape(a.shape, a.dtype) for a in outs),
        in_specs=(vmem,) * 9,
        out_specs=(hbm,) * 9,
        scratch_shapes=[dma((9,))],
        compiler_params=pltpu.CompilerParams(vmem_limit_bytes=8 * 1024 * 1024),
    )(*outs)
    new_w, new_m, fs, ss, nfr, nfc, nsr, nsc, keys = done
    return new_w, new_m, fs[None], ss[None], nfr, nfc, nsr, nsc, keys[None]


def solution(mesh):
    return jax.shard_map(
        local,
        mesh=mesh,
        in_specs=(
            P("grp", "fsdp", None), P("grp", "fsdp", None), P("fsdp", None), P("fsdp", None),
            P("grp", "fsdp", None), P("grp", "fsdp"), P("grp", None), P("grp", "fsdp"),
            P("grp", None),
        ),
        out_specs=(
            P("fsdp", None), P("fsdp", None), P("grp", "fsdp", None), P("grp", "fsdp", None),
            P("grp", "fsdp"), P("grp", None), P("grp", "fsdp"), P("grp", None),
            P("grp", "fsdp", None),
        ),
        check_vma=False,
    )
```

time: 122 us -> 99.5 us (0.82)
  Pallas kernels: 121 us -> 98.7 us
    pallas_call x2, Pallas kernels: 121 us -> 98.7 us  [the longest x1 96.2 us: local(): pl.pallas_call(functools.partial(kernel, n, G, stages), out_shape=(pltpu....]
where the time goes in v1:
time: 99.5 us; the launch traced here: 99.4 us
  Pallas kernels  98.7 us (99%)
    pallas_call x1, Pallas kernels, local(): pl.pallas_call(functools.partial(kernel, n, G, stages), out_shape=(pltpu....  96.2 us
    pallas_call x1, Pallas kernels, local(): pl.pallas_call(finish, out_shape=tuple((shape(a.shape, a.dtype) for a in...  2.54 us

profile of v1, /device:TPU:1, one launch (start us, length us, event | category | flops | bytes accessed | tf_op | source)
XLA Modules:
  0.0 99.4 jit_solution(15375978854836423927)
XLA Ops:
  0.6 96.2 %shard_map.160 = (f32[512,768]{1,0:T(8,128)S(1)}, f32[512,768]{1,0:T(8,128)S(1)}, bf16[512,768]{1,0:T(8,128)(2,1)S(1)}, bf16[512,768]{1,0:T(8,128)(2,1)S(1)}, f3...) custom-call(bf16[512,2048]{1,0:T(8,128)(2,1)} %bitcast.6, ...), custom_call_target="tpu_custom_call" | custom-call | tf_op jit(solution)/shard_map/pallas_call | solution.py:567
  96.8 2.5 %shard_map.161 = (f32[512,768]{1,0:T(8,128)}, f32[512,768]{1,0:T(8,128)}, bf16[512,768]{1,0:T(8,128)(2,1)}, bf16[512,768]{1,0:T(8,128)(2,1)}, f32[1,512]{1,0:T(1...) custom-call(f32[512,768]{1,0:T(8,128)S(1)} %get-tuple-element.27.refs_0_, ...), custom_call_target="tpu_custom_call" | custom-call | tf_op jit(solution)/shard_map/pallas_call | solution.py:599

commit v2 on v1

v2 whole, which is shorter than its diff:
```python
import functools
import typing
import jax
import jax.numpy as jnp
from jax import lax
from jax.experimental import pallas as pl
from jax.experimental.pallas import tpu as pltpu
from jax.sharding import PartitionSpec as P

MESH = pl.DeviceIdType.MESH
f32, bf16 = jnp.float32, jnp.bfloat16
beta_one = 0.9
beta_two = 0.95
bias_one = 1.0 - 0.9**10
bias_two = 1.0 - 0.95**10
adam_eps = 1e-08
inner_rate = 0.01
weight_decay = 0.1
outer_rate = 0.7
outer_beta = 0.9
stat_eps = 1e-06
TILE = 16
UNIT = 128
LAST = [64, 64]
NEAR = 2

class Stage(typing.NamedTuple):
    o: int
    R: int
    PR: int
    PC: int
    nc: int
    NP: int


def plan(rows, C, G):
    sizes = [UNIT] * (rows // UNIT - 1) + LAST
    stages, o = [], 0
    for R in sizes:
        PR = max(TILE, R // G)
        nc = max(k for k in (1, 2, 3, 6) if k == 1 or (R // PR * k <= G and C % (128 * k) == 0))
        stages.append(Stage(o, R, PR, C // nc, nc, R // PR * nc))
        o += R
    return stages


def to_column(row):
    return jnp.broadcast_to(row, (128, row.shape[1])).T


def kernel(
    n, G, stages,
    x_hbm, c_hbm, w_hbm, m_hbm, q_hbm, frm_hbm, fcm_hbm, srm_hbm, scm_hbm,
    o_w, o_m, o_fs, o_ss, o_frm, o_fcm, o_srm, o_scm, o_k,
    x, ct, w, m, q, frm, fcm, srm, scm,
    tb, rb, pb, rp, av, wo, wf, fn, sn, acc, keys, fcol, scol, frn, srn, ca, cb, cmb,
    ld, ts, tr, ps, pr, zs, zf, gr, hs, hr, hm, cs, cr,
):
    g = lax.axis_index("grp")
    z = lax.axis_index("fsdp")
    S = len(stages)
    rows, C = w.shape
    h = lax.rem(g, 2)
    mate = g + 1 - 2 * h
    other_z = lax.rem(z + 1, n)
    cut = rows - UNIT
    lanes = [pl.ds(k, 128) for k in range(0, C, 128)]

    loads = [
        pltpu.make_async_copy(src, dst, ld.at[i])
        for i, (src, dst) in enumerate((
            (c_hbm, ct), (x_hbm, x), (frm_hbm, frm), (fcm_hbm, fcm), (srm_hbm, srm),
            (scm_hbm, scm), (q_hbm, q), (w_hbm, w), (m_hbm, m),
        ))
    ]
    barrier = pltpu.get_barrier_semaphore()
    for d in range(1, n):
        pl.semaphore_signal(
            barrier, inc=1, device_id=(g, lax.rem(z + d, n)), device_id_type=MESH
        )
    for d in range(1, G):
        pl.semaphore_signal(
            barrier, inc=1, device_id=(lax.rem(g + d, G), z), device_id_type=MESH
        )
    for load in loads:
        load.start()
    ca[...] = jnp.zeros_like(ca)
    cb[...] = jnp.zeros_like(cb)
    loads[0].wait()
    loads[1].wait()
    with jax.named_scope("barrier"):
        pl.semaphore_wait(barrier, G - 1 + n - 1)

    def term(c, s):
        st = stages[s]
        lead = st.o % UNIT
        columns = pl.ds(pl.multiple_of(c * rows + (st.o - lead), UNIT), UNIT)
        whole = lax.dot_general(
            x[:, columns], ct[...], (((0,), (0,)), ((), ())), preferred_element_type=f32
        )
        return whole[lead : lead + st.R]

    def block(s):
        return pl.ds(stages[s].o, stages[s].R)

    def move(s, c, slot, to):
        return pltpu.make_async_remote_copy(
            src_ref=tb.at[c, block(s)], dst_ref=rb.at[slot, block(s)], send_sem=ts,
            recv_sem=tr.at[s, slot], device_id=(g, to), device_id_type=MESH,
        )

    def forward(s, k):
        R = stages[s].R
        low = 2 * z < n
        nr = n - 1 - z
        right = jnp.where(low, jnp.where(k < nr, 1, 0), jnp.where(k < z, 0, 1)) == 1
        c = jnp.where(
            low, jnp.where(k < nr, n - 1 - k, k - nr), jnp.where(k < z, k, n - 1 - k + z)
        )
        to = jnp.where(right, z + 1, z - 1)
        slot = jnp.where(jnp.where(right, -1, z - 1) == c, n, c)
        acc[pl.ds(0, R), :] = term(c, s)

        @pl.when(jnp.where(right, z, n - 1 - z) == 0)
        def _():
            tb[c, block(s), :] = acc[pl.ds(0, R), :].astype(bf16)

        @pl.when(jnp.where(right, z, n - 1 - z) > 0)
        def _():
            move(s, c, c, other_z).wait_recv()
            tb[c, block(s), :] = (acc[pl.ds(0, R), :] + rb[c, block(s), :].astype(f32)).astype(bf16)

        move(s, c, slot, to).start()

    def between(body):
        @pl.when((z > 0) & (z < n - 1))
        def _():
            body()

    def at_ends(body):
        @pl.when((z == 0) | (z == n - 1))
        def _():
            body()

    def place_of(s, p):
        st = stages[s]
        return (
            pl.ds(pl.multiple_of(st.o + p // st.nc * st.PR, TILE), st.PR),
            pl.ds(pl.multiple_of(lax.rem(p, st.nc) * st.PC, 128), st.PC),
        )

    def piece(s, p, to):
        st = stages[s]
        return pltpu.make_async_remote_copy(
            src_ref=pb.at[place_of(s, p)],
            dst_ref=rp.at[s, g, pl.ds(0, st.PR), pl.ds(0, st.PC)], send_sem=ps.at[s],
            recv_sem=pr.at[s], device_id=(to, z), device_id_type=MESH,
        )

    def pieces(s, k, sem):
        st = stages[s]
        several = rp.at[s, pl.ds(0, k), pl.ds(0, st.PR), pl.ds(0, st.PC)]
        return pltpu.make_async_copy(several, several, sem)

    def pieces_but_own(s, sem, count=None):
        st = stages[s]
        count = st.NP if count is None else count

        @pl.when(g < st.NP)
        def _():
            pieces(s, count - 1, sem).wait()

        if st.NP < G:
            @pl.when(g >= st.NP)
            def _():
                pieces(s, count, sem).wait()

    def inner(s):
        st = stages[s]
        R = st.R
        acc[pl.ds(0, R), :] = term(z, s)

        @pl.when(z > 0)
        def _():
            move(s, z, z, other_z).wait_recv()
            acc[pl.ds(0, R), :] += rb[z, block(s), :].astype(f32)

        @pl.when(z < n - 1)
        def _():
            move(s, z, n, other_z).wait_recv()
            acc[pl.ds(0, R), :] += rb[n, block(s), :].astype(f32)

        def tile(i, carry):
            at = pl.ds(pl.multiple_of(i * TILE, TILE), TILE)
            place = pl.ds(pl.multiple_of(st.o + i * TILE, TILE), TILE)
            first_row, second_row = fcol[place, :], scol[place, :]
            first_top, second_top = None, None
            for lane in lanes:
                gradient = acc[at, lane]
                codes = q[place, lane]
                first_code = (codes >> 4).astype(f32)
                second_code = (codes & 15).astype(f32) + 1.0
                first_new = (
                    jnp.minimum(first_row, fcm[:, lane]) * (first_code - 7.5)
                    + (1.0 - beta_one) * gradient
                )
                second_new = (
                    jnp.minimum(second_row, scm[:, lane]) * (second_code * second_code)
                    + (1.0 - beta_two) * gradient * gradient
                )
                fn[place, lane] = first_new
                sn[place, lane] = second_new
                update = (first_new * (inner_rate / bias_one)) / (
                    jnp.sqrt(second_new * (1.0 / bias_two)) + adam_eps
                )
                pseudo = update + (inner_rate * weight_decay) * w[place, lane].astype(f32)
                pb[place, lane] = pseudo.astype(bf16)
                size = jnp.abs(first_new)
                ca[:, lane] = jnp.maximum(ca[:, lane], size)
                cb[:, lane] = jnp.maximum(cb[:, lane], second_new)
                first_top = size if first_top is None else jnp.maximum(first_top, size)
                second_top = second_new if second_top is None else jnp.maximum(second_top, second_new)
            frn[place, :] = first_top
            srn[place, :] = second_top
            return carry

        lax.fori_loop(0, R // TILE, tile, 0)

        def send(d, carry):
            p = lax.rem(g + d, G)

            @pl.when(p < st.NP)
            def _():
                piece(s, p, p).start()

            return carry

        lax.fori_loop(1, G, send, 0)

    def plane_copy(s, c, p, to, sem):
        here = (av if c is None else wf.at[c]).at[place_of(s, p)]
        key = z if c is None else c
        return pltpu.make_async_remote_copy(
            src_ref=here, dst_ref=here, send_sem=hs.at[s, key],
            recv_sem=sem.at[s, key], device_id=(to, z), device_id_type=MESH,
        )

    def share(s, c):
        def send(d, carry):
            plane_copy(s, c, g, lax.rem(g + 2 * d, G), hr).start()
            return carry

        lax.fori_loop(1, G // 2, send, 0)
        plane_copy(s, c, g, mate, hm).start()

    def hand(s, c):
        st = stages[s]
        pieces_but_own(s, hr.at[s, z if c is None else c], st.NP // 2)

        def send(d, carry):
            p = lax.rem(g + 2 * d, G)

            @pl.when(p < st.NP)
            def _():
                plane_copy(s, c, p, mate, hm).start()

            return carry

        lax.fori_loop(1, G // 2, send, 0)

    def arrived(s, c):
        pieces(s, stages[s].NP // 2, hm.at[s, z if c is None else c]).wait()

    def reduce(s):
        st = stages[s]
        top = (pl.ds(0, st.PR), pl.ds(0, st.PC))

        @pl.when(g < st.NP)
        def _():
            pieces(s, G - 1, pr.at[s]).wait()
            acc[top] = pb[place_of(s, g)].astype(f32)

            def add(d, carry):
                acc[top] += rp[(s, lax.rem(g + d, G)) + top].astype(f32)
                return carry

            lax.fori_loop(1, G, add, 0)
            averaged = (acc[top] * (1.0 / G)).astype(bf16)
            av[place_of(s, g)] = averaged
            averaged = averaged.astype(f32)
            momentum = outer_beta * m[place_of(s, g)] + averaged
            fresh = w[place_of(s, g)].astype(f32) - outer_rate * (averaged + outer_beta * momentum)
            wo[(s,) + top] = fresh.astype(bf16)

            if s < NEAR:
                between(lambda: to_planes(s))

                @pl.when(z == 0)
                def _():
                    own_piece(s, z + 1).start()

                @pl.when(z == n - 1)
                def _():
                    own_piece(s, z - 1).start()
            else:
                to_planes(s)

            share(s, None)

    def own_piece(s, to):
        st = stages[s]
        return pltpu.make_async_remote_copy(
            src_ref=wo.at[s, pl.ds(0, st.PR), pl.ds(0, st.PC)],
            dst_ref=wf.at[(z,) + place_of(s, g)], send_sem=zs.at[s],
            recv_sem=gr.at[s, z], device_id=(g, to), device_id_type=MESH,
        )

    def to_planes(s):
        for d in range(1, n):
            own_piece(s, lax.rem(z + d, n)).start()

    def passed(s, c, to):
        here = wf.at[(c,) + place_of(s, g)]
        return pltpu.make_async_remote_copy(
            src_ref=here, dst_ref=here, send_sem=zf.at[s],
            recv_sem=gr.at[s, c], device_id=(g, to), device_id_type=MESH,
        )

    def spread(s, c):
        @pl.when(g < stages[s].NP)
        def _():
            passed(s, c, other_z).wait_recv()
            if s < NEAR:
                @pl.when((c == 0) & (z == 1))
                def _():
                    for to in range(2, n):
                        passed(s, c, to).start()

                @pl.when((c == n - 1) & (z == n - 2))
                def _():
                    for to in range(n - 2):
                        passed(s, c, to).start()

            share(s, c)

    def over_mid(body, s):
        def step(c, carry):
            @pl.when(c != z)
            def _():
                body(s, c)

            return carry

        lax.fori_loop(1, n - 1, step, 0)

    def over_near(body, s):
        if n > 2:
            @pl.when(z == 1)
            def _():
                body(s, 0)

            @pl.when(z == n - 2)
            def _():
                body(s, n - 1)

    def over_far(body, s):
        @pl.when((z != 0) & ((z != 1) | (n == 2)))
        def _():
            body(s, 0)

        @pl.when((z != n - 1) & ((z != n - 2) | (n == 2)))
        def _():
            body(s, n - 1)

    def outer(s):
        st = stages[s]
        arrived(s, None)

        def tile(i, carry):
            place = pl.ds(pl.multiple_of(st.o + i * TILE, TILE), TILE)
            averaged = av[place, :].astype(f32)
            momentum = outer_beta * m[place, :] + averaged
            fresh = w[place, :].astype(f32) - outer_rate * (averaged + outer_beta * momentum)
            o_m[place, :] = momentum
            o_w[place, :] = fresh
            wf[z, place, :] = fresh.astype(bf16)
            return carry

        lax.fori_loop(0, st.R // TILE, tile, 0)
    def turn(s, k):
        at = s + k / max(1, n - 2)
        return at - 0.99 if s == S - 1 and k < n - 2 else at

    order = sorted((turn(s, k), k, s) for s in range(S) for k in range(n - 1))

    def send_group(first, last):
        @at_ends
        def _():
            for at, k, s in order:
                if first <= at < last:
                    forward(s, k)

    done = set()

    def once(name, body, *key):
        if min(key[:1]) >= 0 and (name, key) not in done:
            done.add((name, key))
            with jax.named_scope(f"{name}{'_'.join(str(k) for k in key if isinstance(k, int))}"):
                body()

    def do(over, body, t):
        once(body.__name__ + over.__name__[4:], lambda: over(body, t), t)

    paced = S > 3
    send_group(0, 2 if paced else S + 1)

    for load in loads[2:]:
        load.wait()
    fcm[...] = fcm[...] * (beta_one / 7.5)
    scm[...] = scm[...] * (beta_two / 256.0)
    for o in range(0, rows, UNIT):
        part = pl.ds(o, UNIT)
        fcol[part, :] = to_column(frm[:, part] * (beta_one / 7.5))
        scol[part, :] = to_column(srm[:, part] * (beta_two / 256.0))

    def column_max(slot, to):
        return pltpu.make_async_remote_copy(
            src_ref=cmb.at[z], dst_ref=cmb.at[z], send_sem=cs,
            recv_sem=cr, device_id=(g, to), device_id_type=MESH,
        )

    def all_column_max(sem):
        several = cmb.at[pl.ds(0, n - 1)]
        return pltpu.make_async_copy(several, several, sem)

    def forward_rest(s):
        def step(k, carry):
            forward(s, k)
            return carry

        lax.fori_loop(1, n - 1, step, 0)

    def row_max(s):
        part = block(s)
        first = jnp.max(frn[part, :], axis=1, keepdims=True) + stat_eps
        second = jnp.max(srn[part, :], axis=1, keepdims=True) + stat_eps
        frn[part, :] = jnp.broadcast_to(first, (stages[s].R, 128))
        srn[part, :] = jnp.broadcast_to(second, (stages[s].R, 128))

    def rows_out():
        for o in range(0, rows, UNIT):
            part = pl.ds(o, UNIT)
            o_frm[:, part] = frn[part, :].T[:1, :]
            o_srm[:, part] = srn[part, :].T[:1, :]

    for s in range(S):
        last = s == S - 1
        with jax.named_scope(f"fwA{s}"):
            between(functools.partial(forward, s, 0))
        if last:
            with jax.named_scope(f"fwB{s}"):
                between(functools.partial(forward_rest, s))
        if s >= 1:
            with jax.named_scope(f"inner{s-1}"):
                inner(s - 1)
        if last:
            break
        do(over_mid, spread, s - 2)
        if s - 2 < NEAR:
            do(over_near, spread, s - 2)
        if s - 3 < NEAR:
            do(over_far, spread, s - 3)
        once("handav", lambda: hand(s - 2, None), s - 2)
        do(over_mid, hand, s - 3)
        if s - 3 < NEAR:
            do(over_near, hand, s - 3)
        if s - 4 < NEAR:
            do(over_far, hand, s - 4)
        if s >= 1:
            row_max(s - 1)
        with jax.named_scope(f"fwB{s}"):
            between(functools.partial(forward_rest, s))
        once("reduce", lambda: reduce(s - 1), s - 1)
        once("outer", lambda: outer(s - 2), s - 2)
        if paced and s in (1, 2):
            with jax.named_scope(f"group{s+1}"):
                send_group(s + 1, s + 2 if s == 1 else S + 1)

    def last_inner():
        inner(S - 1)
        cmb[z, pl.ds(0, 1), :] = jnp.max(ca[...], axis=0, keepdims=True)
        cmb[z, pl.ds(1, 1), :] = jnp.max(cb[...], axis=0, keepdims=True)
        for d in range(1, n):
            column_max(d, lax.rem(z + d, n)).start()

    def states():
        all_column_max(cr).wait()
        scales = jnp.max(cmb[...], axis=0) + stat_eps
        o_fcm[...] = scales[0:1]
        o_scm[...] = scales[1:2]
        fcm[...] = 1.0 / o_fcm[...]
        scm[...] = 1.0 / o_scm[...]

        def tile(i, carry):
            place = pl.ds(pl.multiple_of(i * TILE, TILE), TILE)
            first_row, second_row = 1.0 / frn[place, :], 1.0 / srn[place, :]
            for lane in lanes:
                o_fs[place, lane] = (fn[place, lane] * jnp.maximum(first_row, fcm[:, lane])).astype(bf16)
                o_ss[place, lane] = (sn[place, lane] * jnp.maximum(second_row, scm[:, lane])).astype(bf16)
            return carry

        lax.fori_loop(0, rows // TILE, tile, 0)

    def product(c, o, width):
        columns = pl.ds(pl.multiple_of(c * rows + o, UNIT), width)
        return jnp.dot(x[:, columns], wf[c, pl.ds(o, width), :], preferred_element_type=f32)

    def others(body):
        def step(j, carry):
            for c in (z - j, z + j):
                @pl.when((c >= 0) & (c < n))
                def _():
                    body(c)

            return carry

        lax.fori_loop(1, n, step, 0)

    def gather_early(c):
        for s in range(S - 2):
            arrived(s, c)
        keys[...] += product(c, 0, cut)

    def gather_mid(c):
        @pl.when((c > 0) & (c < n - 1))
        def _():
            gather_early(c)

    def gather_end(c):
        @pl.when((c == 0) | (c == n - 1))
        def _():
            gather_early(c)

    def own():
        if cut:
            keys[...] = product(z, 0, cut)
        else:
            keys[...] = jnp.zeros_like(keys)

    def run(name, body):
        with jax.named_scope(name):
            body()

    everywhere = (over_mid, over_near, over_far)
    run("lastinner", last_inner)
    once("reduce", lambda: reduce(S - 2), S - 2)
    row_max(S - 2)
    row_max(S - 1)
    run("rowsout", rows_out)
    for t in range(S - 2):
        for over in everywhere:
            do(over, spread, t)
    for t in range(S - 2):
        once("handav", functools.partial(hand, t, None), t)
        once("outer", functools.partial(outer, t), t)
    run("own", own)
    once("reduce", lambda: reduce(S - 1), S - 1)
    for over in everywhere:
        do(over, spread, S - 2)
    for t in range(S - 2):
        for over in everywhere:
            do(over, hand, t)
    once("handav", lambda: hand(S - 2, None), S - 2)
    run("states", states)
    if cut:
        run("gmid", functools.partial(others, gather_mid))
    for over in everywhere:
        do(over, spread, S - 1)
    for over in everywhere:
        do(over, hand, S - 2)
    once("outer", lambda: outer(S - 2), S - 2)
    once("handav", lambda: hand(S - 1, None), S - 1)
    if cut:
        run("gend", functools.partial(others, gather_end))
    once("outer", lambda: outer(S - 1), S - 1)
    for over in everywhere:
        do(over, hand, S - 1)

    def last_pieces(c):
        for s in (S - 2, S - 1):
            arrived(s, c)

    run("lastpieces", functools.partial(others, last_pieces))

    def last_product():
        TT = UNIT

        def tile(i, carry):
            tokens = pl.ds(pl.multiple_of(i * TT, TT), TT)
            total = keys[tokens, :]
            for c in range(n):
                total += jnp.dot(
                    x[tokens, pl.ds(c * rows + cut, UNIT)], wf[c, pl.ds(cut, UNIT), :],
                    preferred_element_type=f32,
                )
            o_k[tokens, :] = total.astype(bf16)
            return carry

        lax.fori_loop(0, x.shape[0] // TT, tile, 0)

    run("lastprod", last_product)

    def sends():
        chunks = tb.at[pl.ds(0, n - 1)]
        pltpu.make_async_copy(chunks, chunks, ts).wait()

        for s in range(S):
            pieces_but_own(s, ps.at[s])

        def chunk(c, carry):
            for s in range(S):
                half = stages[s].NP // 2

                @pl.when(g < stages[s].NP)
                def _():
                    pieces(s, G // 2 + half - 1, hs.at[s, c]).wait()

                if stages[s].NP < G:
                    @pl.when(g >= stages[s].NP)
                    def _():
                        pieces(s, half, hs.at[s, c]).wait()

            return carry

        lax.fori_loop(0, n, chunk, 0)
        for s in range(S):
            @pl.when(g < stages[s].NP)
            def _():
                if s >= NEAR:
                    pieces(s, n - 1, zs.at[s]).wait()
                else:
                    between(lambda: pieces(s, n - 1, zs.at[s]).wait())
                    at_ends(lambda: pieces(s, 1, zs.at[s]).wait())
                    if n > 3:
                        @pl.when((z == 1) | (z == n - 2))
                        def _():
                            pieces(s, n - 2, zf.at[s]).wait()

        all_column_max(cs).wait()

    run("sends", sends)


def finish(*refs):
    k = (len(refs) - 1) // 2
    sems = refs[-1]
    copies = [
        pltpu.make_async_copy(src, dst, sems.at[i])
        for i, (src, dst) in enumerate(zip(refs[:k], refs[k:-1]))
    ]
    for copy in copies:
        copy.start()
    for copy in copies:
        copy.wait()


def local(x, ct, w, m, q, frm, fcm, srm, scm):
    n, G = lax.axis_size("fsdp"), lax.axis_size("grp")
    rows, C = w.shape
    T, K = x.shape[1:]
    stages = plan(rows, C, G)
    S = len(stages)
    PR = max(st.PR for st in stages)
    hbm = pl.BlockSpec(memory_space=pltpu.HBM)
    vmem = pl.BlockSpec(memory_space=pltpu.VMEM)
    dma = pltpu.SemaphoreType.DMA
    shape = jax.ShapeDtypeStruct
    outs = pl.pallas_call(
        functools.partial(kernel, n, G, stages),
        out_shape=(
            pltpu.VMEM((rows, C), f32), pltpu.VMEM((rows, C), f32),
            pltpu.VMEM((rows, C), bf16), pltpu.VMEM((rows, C), bf16),
            pltpu.VMEM((1, rows), f32), pltpu.VMEM((1, C), f32),
            pltpu.VMEM((1, rows), f32), pltpu.VMEM((1, C), f32),
            pltpu.VMEM((T, C), bf16),
        ),
        in_specs=[hbm] * 9,
        out_specs=(vmem,) * 9,
        scratch_shapes=[
            pltpu.VMEM((T, K), bf16), pltpu.VMEM((T, C), bf16), pltpu.VMEM((rows, C), bf16),
            pltpu.VMEM((rows, C), f32), pltpu.VMEM((rows, C), jnp.int32),
            pltpu.VMEM((1, rows), f32), pltpu.VMEM((1, C), f32),
            pltpu.VMEM((1, rows), f32), pltpu.VMEM((1, C), f32),
            pltpu.VMEM((n, rows, C), bf16), pltpu.VMEM((n + 1, rows, C), bf16),
            pltpu.VMEM((rows, C), bf16), pltpu.VMEM((S, G, PR, C), bf16),
            pltpu.VMEM((rows, C), bf16), pltpu.VMEM((S, PR, C), bf16), pltpu.VMEM((n, rows, C), bf16),
            pltpu.VMEM((rows, C), f32), pltpu.VMEM((rows, C), f32),
            pltpu.VMEM((UNIT, C), f32), pltpu.VMEM((T, C), f32),
            pltpu.VMEM((rows, 128), f32), pltpu.VMEM((rows, 128), f32),
            pltpu.VMEM((rows, 128), f32), pltpu.VMEM((rows, 128), f32),
            pltpu.VMEM((TILE, C), f32), pltpu.VMEM((TILE, C), f32), pltpu.VMEM((n, 2, C), f32),
            dma((9,)), dma, dma((S, n + 1)), dma((S,)), dma((S,)), dma((S,)), dma((S,)),
            dma((S, n)), dma((S, n)), dma((S, n)), dma((S, n)), dma, dma,
        ],
        compiler_params=pltpu.CompilerParams(
            collective_id=0, has_side_effects=True, vmem_limit_bytes=54 * 1024 * 1024
        ),
    )(x[0], ct[0], w, m, q[0], frm, fcm, srm, scm)
    done = pl.pallas_call(
        finish,
        out_shape=tuple(shape(a.shape, a.dtype) for a in outs),
        in_specs=(vmem,) * 9,
        out_specs=(hbm,) * 9,
        scratch_shapes=[dma((9,))],
        compiler_params=pltpu.CompilerParams(vmem_limit_bytes=8 * 1024 * 1024),
    )(*outs)
    new_w, new_m, fs, ss, nfr, nfc, nsr, nsc, keys = done
    return new_w, new_m, fs[None], ss[None], nfr, nfc, nsr, nsc, keys[None]


def solution(mesh):
    return jax.shard_map(
        local,
        mesh=mesh,
        in_specs=(
            P("grp", "fsdp", None), P("grp", "fsdp", None), P("fsdp", None), P("fsdp", None),
            P("grp", "fsdp", None), P("grp", "fsdp"), P("grp", None), P("grp", "fsdp"),
            P("grp", None),
        ),
        out_specs=(
            P("fsdp", None), P("fsdp", None), P("grp", "fsdp", None), P("grp", "fsdp", None),
            P("grp", "fsdp"), P("grp", None), P("grp", "fsdp"), P("grp", None),
            P("grp", "fsdp", None),
        ),
        check_vma=False,
    )
```

time: 99.5 us -> 85.1 us (0.86)
  Pallas kernels: 98.7 us -> 84.3 us
    pallas_call x1, Pallas kernels: 96.2 us -> 81.8 us  [local(): pl.pallas_call(functools.partial(kernel, n, G, stages), out_shape=(pltpu....]
where the time goes in v2:
time: 85.1 us; the launch traced here: 85 us
  Pallas kernels  84.3 us (99%)
    pallas_call x1, Pallas kernels, local(): pl.pallas_call(functools.partial(kernel, n, G, stages), out_shape=(pltpu....  81.8 us
    pallas_call x1, Pallas kernels, local(): pl.pallas_call(finish, out_shape=tuple((shape(a.shape, a.dtype) for a in...  2.54 us

profile of v2, /device:TPU:1, one launch (start us, length us, event | category | flops | bytes accessed | tf_op | source)
XLA Modules:
  0.0 85.0 jit_solution(3414288637419647750)
XLA Ops:
  0.6 81.8 %shard_map.160 = (f32[512,768]{1,0:T(8,128)S(1)}, f32[512,768]{1,0:T(8,128)S(1)}, bf16[512,768]{1,0:T(8,128)(2,1)S(1)}, bf16[512,768]{1,0:T(8,128)(2,1)S(1)}, f3...) custom-call(bf16[512,2048]{1,0:T(8,128)(2,1)} %bitcast.6, ...), custom_call_target="tpu_custom_call" | custom-call | tf_op jit(solution)/shard_map/pallas_call | solution.py:678
  82.5 2.5 %shard_map.161 = (f32[512,768]{1,0:T(8,128)}, f32[512,768]{1,0:T(8,128)}, bf16[512,768]{1,0:T(8,128)(2,1)}, bf16[512,768]{1,0:T(8,128)(2,1)}, f32[1,512]{1,0:T(1...) custom-call(f32[512,768]{1,0:T(8,128)S(1)} %get-tuple-element.27.refs_0_, ...), custom_call_target="tpu_custom_call" | custom-call | tf_op jit(solution)/shard_map/pallas_call | solution.py:709

commit v3 on v2

--- a/solution.py
+++ b/solution.py
@@ -64,6 +64,7 @@
     mate = g + 1 - 2 * h
     other_z = lax.rem(z + 1, n)
     cut = rows - UNIT
+    held = S - 3
     lanes = [pl.ds(k, 128) for k in range(0, C, 128)]
 
     loads = [
@@ -88,9 +89,6 @@
     cb[...] = jnp.zeros_like(cb)
     loads[0].wait()
     loads[1].wait()
-    with jax.named_scope("barrier"):
-        pl.semaphore_wait(barrier, G - 1 + n - 1)
-
     def term(c, s):
         st = stages[s]
         lead = st.o % UNIT
@@ -109,7 +107,7 @@
             recv_sem=tr.at[s, slot], device_id=(g, to), device_id_type=MESH,
         )
 
-    def forward(s, k):
+    def forward(s, k, ready=False):
         R = stages[s].R
         low = 2 * z < n
         nr = n - 1 - z
@@ -119,16 +117,17 @@
         )
         to = jnp.where(right, z + 1, z - 1)
         slot = jnp.where(jnp.where(right, -1, z - 1) == c, n, c)
-        acc[pl.ds(0, R), :] = term(c, s)
-
-        @pl.when(jnp.where(right, z, n - 1 - z) == 0)
-        def _():
-            tb[c, block(s), :] = acc[pl.ds(0, R), :].astype(bf16)
-
-        @pl.when(jnp.where(right, z, n - 1 - z) > 0)
-        def _():
-            move(s, c, c, other_z).wait_recv()
-            tb[c, block(s), :] = (acc[pl.ds(0, R), :] + rb[c, block(s), :].astype(f32)).astype(bf16)
+        if not ready:
+            acc[pl.ds(0, R), :] = term(c, s)
+
+            @pl.when(jnp.where(right, z, n - 1 - z) == 0)
+            def _():
+                tb[c, block(s), :] = acc[pl.ds(0, R), :].astype(bf16)
+
+            @pl.when(jnp.where(right, z, n - 1 - z) > 0)
+            def _():
+                move(s, c, c, other_z).wait_recv()
+                tb[c, block(s), :] = (acc[pl.ds(0, R), :] + rb[c, block(s), :].astype(f32)).astype(bf16)
 
         move(s, c, slot, to).start()
 
@@ -241,7 +240,7 @@
         here = (av if c is None else wf.at[c]).at[place_of(s, p)]
         key = z if c is None else c
         return pltpu.make_async_remote_copy(
-            src_ref=here, dst_ref=here, send_sem=hs.at[s, key],
+            src_ref=here, dst_ref=here, send_sem=hs.at[s],
             recv_sem=sem.at[s, key], device_id=(to, z), device_id_type=MESH,
         )
 
@@ -302,6 +301,8 @@
                 @pl.when(z == n - 1)
                 def _():
                     own_piece(s, z - 1).start()
+            elif s == held:
+                pass
             else:
                 to_planes(s)
 
@@ -398,7 +399,7 @@
         def _():
             for at, k, s in order:
                 if first <= at < last:
-                    forward(s, k)
+                    forward(s, k, ready=(s, k) == (0, 0))
 
     done = set()
 
@@ -411,6 +412,14 @@
     def do(over, body, t):
         once(body.__name__ + over.__name__[4:], lambda: over(body, t), t)
 
+    far = jnp.where(2 * z < n, n - 1, 0)
+
+    @at_ends
+    def _():
+        tb[far, block(0), :] = term(far, 0).astype(bf16)
+
+    with jax.named_scope("barrier"):
+        pl.semaphore_wait(barrier, G - 1 + n - 1)
     paced = S > 3
     send_group(0, 2 if paced else S + 1)
 
@@ -453,18 +462,20 @@
             o_frm[:, part] = frn[part, :].T[:1, :]
             o_srm[:, part] = srn[part, :].T[:1, :]
 
-    for s in range(S):
-        last = s == S - 1
-        with jax.named_scope(f"fwA{s}"):
-            between(functools.partial(forward, s, 0))
-        if last:
-            with jax.named_scope(f"fwB{s}"):
-                between(functools.partial(forward_rest, s))
+    def far_chunk(s):
+        once("fwA", lambda: between(functools.partial(forward, s, 0)), s)
+
+    def near_chunks(s):
+        once("fwB", lambda: between(functools.partial(forward_rest, s)), s)
+
+    for s in range(S - 1):
+        far_chunk(s)
+        if s == S - 2 and s - 2 < NEAR:
+            do(over_near, spread, s - 2)
         if s >= 1:
-            with jax.named_scope(f"inner{s-1}"):
-                inner(s - 1)
-        if last:
-            break
+            once("inner", lambda: inner(s - 1), s - 1)
+        if s == S - 2:
+            far_chunk(s + 1)
         do(over_mid, spread, s - 2)
         if s - 2 < NEAR:
             do(over_near, spread, s - 2)
@@ -478,15 +489,38 @@
             do(over_far, hand, s - 4)
         if s >= 1:
             row_max(s - 1)
-        with jax.named_scope(f"fwB{s}"):
-            between(functools.partial(forward_rest, s))
+        near_chunks(s)
         once("reduce", lambda: reduce(s - 1), s - 1)
-        once("outer", lambda: outer(s - 2), s - 2)
+        if s == S - 2:
+            near_chunks(s + 1)
+            if held >= NEAR:
+                @between
+                def _():
+                    @pl.when(g < stages[held].NP)
+                    def _():
+                        to_planes(held)
+            once("outer", lambda: outer(s - 2), s - 2)
+        if s < S - 2:
+            once("outer", lambda: outer(s - 2), s - 2)
         if paced and s in (1, 2):
             with jax.named_scope(f"group{s+1}"):
                 send_group(s + 1, s + 2 if s == 1 else S + 1)
+    once("inner", lambda: inner(S - 2), S - 2)
+    if S - 4 < NEAR:
+        do(over_far, spread, S - 4)
+    once("handav", lambda: hand(S - 3, None), S - 3)
 
     def last_inner():
+        if held >= NEAR:
+            @at_ends
+            def _():
+                chunks = tb.at[pl.ds(0, n - 1)]
+                pltpu.make_async_copy(chunks, chunks, ts).wait()
+
+                @pl.when(g < stages[held].NP)
+                def _():
+                    to_planes(held)
+
         inner(S - 1)
         cmb[z, pl.ds(0, 1), :] = jnp.max(ca[...], axis=0, keepdims=True)
         cmb[z, pl.ds(1, 1), :] = jnp.max(cb[...], axis=0, keepdims=True)
@@ -553,38 +587,37 @@
 
     everywhere = (over_mid, over_near, over_far)
     run("lastinner", last_inner)
+    for t in range(S - 2):
+        for over in everywhere:
+            do(over, spread, t)
     once("reduce", lambda: reduce(S - 2), S - 2)
     row_max(S - 2)
     row_max(S - 1)
     run("rowsout", rows_out)
     for t in range(S - 2):
-        for over in everywhere:
-            do(over, spread, t)
-    for t in range(S - 2):
         once("handav", functools.partial(hand, t, None), t)
         once("outer", functools.partial(outer, t), t)
-    run("own", own)
     once("reduce", lambda: reduce(S - 1), S - 1)
     for over in everywhere:
         do(over, spread, S - 2)
+    once("handav", lambda: hand(S - 2, None), S - 2)
+    run("states", states)
+    run("own", own)
     for t in range(S - 2):
         for over in everywhere:
             do(over, hand, t)
-    once("handav", lambda: hand(S - 2, None), S - 2)
-    run("states", states)
+    for over in everywhere:
+        do(over, spread, S - 1)
+    once("handav", lambda: hand(S - 1, None), S - 1)
+    once("outer", lambda: outer(S - 2), S - 2)
+    for over in everywhere:
+        do(over, hand, S - 2)
     if cut:
         run("gmid", functools.partial(others, gather_mid))
-    for over in everywhere:
-        do(over, spread, S - 1)
-    for over in everywhere:
-        do(over, hand, S - 2)
-    once("outer", lambda: outer(S - 2), S - 2)
-    once("handav", lambda: hand(S - 1, None), S - 1)
-    if cut:
         run("gend", functools.partial(others, gather_end))
-    once("outer", lambda: outer(S - 1), S - 1)
     for over in everywhere:
         do(over, hand, S - 1)
+    once("outer", lambda: outer(S - 1), S - 1)
 
     def last_pieces(c):
         for s in (S - 2, S - 1):
@@ -598,9 +631,12 @@
         def tile(i, carry):
             tokens = pl.ds(pl.multiple_of(i * TT, TT), TT)
             total = keys[tokens, :]
-            for c in range(n):
+            for c in range(0, n, 2):
+                pair = range(c, min(n, c + 2))
+                left = [x[tokens, pl.ds(k * rows + cut, UNIT)] for k in pair]
+                right = [wf[k, pl.ds(cut, UNIT), :] for k in pair]
                 total += jnp.dot(
-                    x[tokens, pl.ds(c * rows + cut, UNIT)], wf[c, pl.ds(cut, UNIT), :],
+                    jnp.concatenate(left, axis=1), jnp.concatenate(right, axis=0),
                     preferred_element_type=f32,
                 )
             o_k[tokens, :] = total.astype(bf16)
@@ -611,28 +647,35 @@
     run("lastprod", last_product)
 
     def sends():
-        chunks = tb.at[pl.ds(0, n - 1)]
-        pltpu.make_async_copy(chunks, chunks, ts).wait()
+        def pieces_sent():
+            chunks = tb.at[pl.ds(0, n - 1)]
+            pltpu.make_async_copy(chunks, chunks, ts).wait()
+
+        if held >= NEAR:
+            between(pieces_sent)
+        else:
+            pieces_sent()
 
         for s in range(S):
             pieces_but_own(s, ps.at[s])
 
-        def chunk(c, carry):
-            for s in range(S):
-                half = stages[s].NP // 2
-
-                @pl.when(g < stages[s].NP)
+        def spread_sent(s, k):
+            st = stages[s]
+            several = rp.at[pl.ds(0, n), pl.ds(0, k), pl.ds(0, st.PR), pl.ds(0, st.PC)]
+            pltpu.make_async_copy(several, several, hs.at[s]).wait()
+
+        for s in range(S):
+            half = stages[s].NP // 2
+
+            @pl.when(g < stages[s].NP)
+            def _():
+                spread_sent(s, G // 2 + half - 1)
+
+            if stages[s].NP < G:
+                @pl.when(g >= stages[s].NP)
                 def _():
-                    pieces(s, G // 2 + half - 1, hs.at[s, c]).wait()
-
-                if stages[s].NP < G:
-                    @pl.when(g >= stages[s].NP)
-                    def _():
-                        pieces(s, half, hs.at[s, c]).wait()
-
-            return carry
-
-        lax.fori_loop(0, n, chunk, 0)
+                    spread_sent(s, half)
+
         for s in range(S):
             @pl.when(g < stages[s].NP)
             def _():
@@ -692,7 +735,7 @@
             pltpu.VMEM((1, rows), f32), pltpu.VMEM((1, C), f32),
             pltpu.VMEM((1, rows), f32), pltpu.VMEM((1, C), f32),
             pltpu.VMEM((n, rows, C), bf16), pltpu.VMEM((n + 1, rows, C), bf16),
-            pltpu.VMEM((rows, C), bf16), pltpu.VMEM((S, G, PR, C), bf16),
+            pltpu.VMEM((rows, C), bf16), pltpu.VMEM((max(S, n), G, PR, C), bf16),
             pltpu.VMEM((rows, C), bf16), pltpu.VMEM((S, PR, C), bf16), pltpu.VMEM((n, rows, C), bf16),
             pltpu.VMEM((rows, C), f32), pltpu.VMEM((rows, C), f32),
             pltpu.VMEM((UNIT, C), f32), pltpu.VMEM((T, C), f32),
@@ -700,7 +743,7 @@
             pltpu.VMEM((rows, 128), f32), pltpu.VMEM((rows, 128), f32),
             pltpu.VMEM((TILE, C), f32), pltpu.VMEM((TILE, C), f32), pltpu.VMEM((n, 2, C), f32),
             dma((9,)), dma, dma((S, n + 1)), dma((S,)), dma((S,)), dma((S,)), dma((S,)),
-            dma((S, n)), dma((S, n)), dma((S, n)), dma((S, n)), dma, dma,
+            dma((S, n)), dma((S,)), dma((S, n)), dma((S, n)), dma, dma,
         ],
         compiler_params=pltpu.CompilerParams(
             collective_id=0, has_side_effects=True, vmem_limit_bytes=54 * 1024 * 1024

time: 85.1 us -> 78.6 us (0.924)
  Pallas kernels: 84.3 us -> 77.7 us
    pallas_call x1, Pallas kernels: 81.8 us -> 75.1 us  [local(): pl.pallas_call(functools.partial(kernel, n, G, stages), out_shape=(pltpu....]
where the time goes in v3:
time: 78.6 us; the launch traced here: 78.5 us
  Pallas kernels  77.7 us (99%)
  between operations  0.81 us (1%)
    pallas_call x1, Pallas kernels, local(): pl.pallas_call(functools.partial(kernel, n, G, stages), out_shape=(pltpu....  75.1 us
    pallas_call x1, Pallas kernels, local(): pl.pallas_call(finish, out_shape=tuple((shape(a.shape, a.dtype) for a in...  2.54 us

profile of v3, /device:TPU:1, one launch (start us, length us, event | category | flops | bytes accessed | tf_op | source)
XLA Modules:
  0.0 78.5 jit_solution(6287480494536497900)
XLA Ops:
  0.6 75.1 %shard_map.160 = (f32[512,768]{1,0:T(8,128)S(1)}, f32[512,768]{1,0:T(8,128)S(1)}, bf16[512,768]{1,0:T(8,128)(2,1)S(1)}, bf16[512,768]{1,0:T(8,128)(2,1)S(1)}, f3...) custom-call(bf16[512,2048]{1,0:T(8,128)(2,1)} %bitcast.6, ...), custom_call_target="tpu_custom_call" | custom-call | tf_op jit(solution)/shard_map/pallas_call | solution.py:721
  75.8 2.5 %shard_map.161 = (f32[512,768]{1,0:T(8,128)}, f32[512,768]{1,0:T(8,128)}, bf16[512,768]{1,0:T(8,128)(2,1)}, bf16[512,768]{1,0:T(8,128)(2,1)}, f32[1,512]{1,0:T(1...) custom-call(f32[512,768]{1,0:T(8,128)S(1)} %get-tuple-element.27.refs_0_, ...), custom_call_target="tpu_custom_call" | custom-call | tf_op jit(solution)/shard_map/pallas_call | solution.py:752
